TPU v7x, 32 devices: a whole 2x2x4 slice. The times are simulated.
32 devices in a mesh: dp: 4 (over x, core), tensor: 8 (over z, y).
Axes of the slice: x: 2, y: 2, z: 4, core: 2. Of those that a mesh axis runs over, the one named last changes fastest.
Arguments:
- head_outputs: bfloat16 [4096, 4096], P('dp', 'tensor'), may hold values from -6 to 6
- out_weight: bfloat16 [4096, 4096], P('tensor'), may hold values from -0.09375 to 0.09375
- residual: bfloat16 [4096, 4096], P(('dp', 'tensor')), may hold values from -6 to 6
- norm_gain: float32 [4096], replicated, may hold values from 0.25 to 1.75
- chosen: int32 [16, 256], replicated, may hold values from 0 to 4095, as said below
- gates: float32 [16, 256], replicated, may hold values from 0.25 to 1
- place: int32 [16], replicated, may hold values from 0 to 15, each once
- w_gate: bfloat16 [32, 704, 4096], P(('dp', 'tensor')), may hold values from -0.09375 to 0.09375
- w_up: bfloat16 [32, 704, 4096], P(('dp', 'tensor')), may hold values from -0.09375 to 0.09375
- w_down: bfloat16 [32, 704, 4096], P(('dp', 'tensor')), may hold values from -0.15625 to 0.15625
Outputs:
- mixed: bfloat16 [4096, 4096], P(('dp', 'tensor'))
Inputs may be any that keep to these rules, and one draw needn't show every extreme that they name: `chosen`: row e lists 256 different tokens; at most 16 of them lie in one aligned block of 128 rows (the rows of one device), and in every row some block holds exactly 16.
All inputs are finite; a program needn't handle non-finite values.
Results may differ from a plain program's by a relative error of at most 0.012.
Values may be sent and summed in bfloat16 or wider, within the bound.
A program may use at most 128 MiB of HBM per device.

v0:
```python
import functools

import jax
import jax.numpy as jnp
from jax import lax
from jax.experimental import pallas as pl
from jax.experimental.pallas import tpu as pltpu
from jax.sharding import PartitionSpec as P

MESH = pl.DeviceIdType.MESH
LANES = 4


def ring_rank(position, count):
    upper = position // (count // 2)
    return (1 - upper) * 2 * position + upper * (2 * (count - 1 - position) + 1)


def project_kernel(count, x_ref, w_ref, out_ref, held, term, send_sem, recv_sem):
    dp = lax.axis_index("dp")
    rank = lax.axis_index("tensor")
    odd = rank % 2
    half = rank // 2
    here = (1 - odd) * half + odd * (count - 1 - half)
    right = ring_rank((here + 1) % count, count)
    left = ring_rank((here + count - 1) % count, count)
    rows = out_ref.shape[0]
    width = out_ref.shape[1] // LANES

    def own_term(lane, block):
        start = pl.multiple_of(ring_rank(block, count) * rows, rows)
        return jnp.dot(
            x_ref[pl.ds(start, rows), :],
            w_ref[:, lane * width : (lane + 1) * width],
            preferred_element_type=jnp.float32,
        )

    def block_of(lane, slot):
        if lane < LANES // 2:
            return (here + 2 * count - 1 - slot) % count
        return (here + 1 + slot) % count

    def copy(lane, slot):
        return pltpu.make_async_remote_copy(
            src_ref=held.at[lane, slot],
            dst_ref=held.at[lane, slot + 1],
            send_sem=send_sem.at[lane, slot],
            recv_sem=recv_sem.at[lane, slot + 1],
            device_id=(dp, right if lane < LANES // 2 else left),
            device_id_type=MESH,
        )

    def arrival(lane, slot):
        return pltpu.make_async_remote_copy(
            src_ref=held.at[lane, slot],
            dst_ref=held.at[lane, slot],
            send_sem=send_sem.at[lane, slot],
            recv_sem=recv_sem.at[lane, slot],
            device_id=(dp, right if lane < LANES // 2 else left),
            device_id_type=MESH,
        )

    order = [lane for k in range(LANES // 2) for lane in (k, LANES // 2 + k)]
    barrier = pltpu.get_barrier_semaphore()
    for neighbour in (left, right):
        pl.semaphore_signal(barrier, inc=1, device_id=(dp, neighbour), device_id_type=MESH)
    for n, lane in enumerate(order):
        held[lane, 0] = own_term(lane, block_of(lane, 0)).astype(held.dtype)
        if n == 0:
            pl.semaphore_wait(barrier, 2)
        copy(lane, 0).start()

    def step(slot, carry):
        for lane in order:
            term[lane] = own_term(lane, block_of(lane, slot))
        for lane in order:
            arrival(lane, slot).wait_recv()
            held[lane, slot] = (held[lane, slot].astype(jnp.float32) + term[lane]).astype(held.dtype)
            copy(lane, slot).start()
        return carry

    lax.fori_loop(1, count - 1, step, 0)
    last = count - 1
    for lane in order:
        term[lane] = own_term(lane, block_of(lane, last))
    for lane in order:
        arrival(lane, last).wait_recv()
        out_ref[:, lane * width : (lane + 1) * width] = (
            held[lane, last].astype(jnp.float32) + term[lane]
        )

    def drain(slot, carry):
        for lane in order:
            copy(lane, slot).wait_send()
        return carry

    lax.fori_loop(0, count - 1, drain, 0)


def project(x, w, count):
    rows = x.shape[0] // count
    columns = w.shape[1]
    width = columns // LANES
    return pl.pallas_call(
        functools.partial(project_kernel, count),
        out_shape=jax.ShapeDtypeStruct((rows, columns), jnp.float32),
        in_specs=[pl.BlockSpec(memory_space=pltpu.VMEM)] * 2,
        out_specs=pl.BlockSpec(memory_space=pltpu.VMEM),
        scratch_shapes=[
            pltpu.VMEM((LANES, count, rows, width), jnp.bfloat16),
            pltpu.VMEM((LANES, rows, width), jnp.float32),
            pltpu.SemaphoreType.DMA((LANES, count)),
            pltpu.SemaphoreType.DMA((LANES, count)),
        ],
        compiler_params=pltpu.CompilerParams(
            collective_id=0, has_side_effects=True, vmem_limit_bytes=48 * 1024 * 1024
        ),
    )(x, w)


class Place:
    def __init__(self, replicas, count):
        self.dp = lax.axis_index("dp")
        rank = lax.axis_index("tensor")
        self.odd = rank % 2
        self.per_row = count // 2
        self.pairs = replicas * self.per_row
        self.pair = self.dp * self.per_row + rank // 2
        self.partner = (self.dp, rank + 1 - 2 * self.odd)

    def device(self, pair):
        return (pair // self.per_row, 2 * (pair % self.per_row) + self.odd)

    def greet(self):
        barrier = pltpu.get_barrier_semaphore()

        def signal(k, carry):
            target = self.device((self.pair + k) % self.pairs)
            pl.semaphore_signal(barrier, inc=1, device_id=target, device_id_type=MESH)
            return carry

        lax.fori_loop(1, self.pairs, signal, 0)
        pl.semaphore_signal(barrier, inc=1, device_id=self.partner, device_id_type=MESH)
        pl.semaphore_wait(barrier, self.pairs)


def loop(start, stop, body):
    def step(k, carry):
        body(k)
        return carry

    lax.fori_loop(start, stop, step, 0)


PIECES = 4


def experts_kernel(
    replicas,
    count,
    group,
    x_ref,
    gate_hbm,
    up_hbm,
    down_hbm,
    out_ref,
    gate_w,
    up_w,
    down_w,
    received,
    result,
    part,
    weight_sem,
    send_sem,
    pass_sem,
    recv_sem,
    cross_sem,
    part_sem,
    home_sem,
    done_sem,
    keep_sem,
):
    at = Place(replicas, count)
    most, width = x_ref.shape[1:]
    rows = group * 2 * most
    groups = at.pairs // group

    def source(k):
        return (at.pair + at.pairs - k) % at.pairs

    def outward(k):
        target = (at.pair + k) % at.pairs
        return pltpu.make_async_remote_copy(
            src_ref=x_ref.at[target],
            dst_ref=received.at[k, at.odd],
            send_sem=send_sem.at[k],
            recv_sem=recv_sem.at[k, at.odd],
            device_id=at.device(target),
            device_id_type=MESH,
        )

    def sideways(k, side):
        return pltpu.make_async_remote_copy(
            src_ref=received.at[k, side],
            dst_ref=received.at[k, side],
            send_sem=pass_sem.at[k],
            recv_sem=recv_sem.at[k, side],
            device_id=at.partner,
            device_id_type=MESH,
        )

    def across(k):
        return pltpu.make_async_remote_copy(
            src_ref=result.at[k, 1 - at.odd],
            dst_ref=part.at[k],
            send_sem=cross_sem.at[k],
            recv_sem=part_sem.at[k],
            device_id=at.partner,
            device_id_type=MESH,
        )

    def home(k):
        return pltpu.make_async_remote_copy(
            src_ref=part.at[k],
            dst_ref=out_ref.at[at.pair],
            send_sem=home_sem.at[k],
            recv_sem=done_sem.at[at.pair],
            device_id=at.device(source(k)),
            device_id_type=MESH,
        )

    def forward(k):
        sideways(k, at.odd).wait_recv()
        sideways(k, at.odd).start()

    def add(k):
        across(k).wait_recv()
        part[k] = (
            part[k].astype(jnp.float32) + result[k, at.odd].astype(jnp.float32)
        ).astype(part.dtype)

    def add_and_send(k):
        add(k)
        home(k).start()

    loads = [
        pltpu.make_async_copy(hbm.at[0], vmem, weight_sem.at[n])
        for n, (hbm, vmem) in enumerate(((gate_hbm, gate_w), (up_hbm, up_w), (down_hbm, down_w)))
    ]
    for load in loads:
        load.start()
    own = pltpu.make_async_remote_copy(
        src_ref=x_ref.at[at.pair],
        dst_ref=received.at[0, at.odd],
        send_sem=pass_sem.at[0],
        recv_sem=recv_sem.at[0, at.odd],
        device_id=at.partner,
        device_id_type=MESH,
    )
    at.greet()
    loop(1, at.pairs, lambda k: outward(k).start())
    own.start()
    received[0, at.odd] = x_ref[at.pair]
    loop(1, group, forward)
    for load in loads:
        load.wait()
    contract = (((1,), (1,)), ((), ()))

    def step(g):
        first = g * group

        def forward_piece(piece):
            @pl.when(g + 1 < groups)
            def _():
                start = first + group
                cut = [start + n * group // PIECES for n in (piece, piece + 1)]
                loop(cut[0], cut[1], forward)

        loop(first, first + group, lambda k: sideways(k, 1 - at.odd).wait_recv())
        x = received[pl.ds(first, group)].reshape(rows, width)
        gate_part = lax.dot_general(x, gate_w[...], contract, preferred_element_type=jnp.float32)
        forward_piece(0)
        up_part = lax.dot_general(x, up_w[...], contract, preferred_element_type=jnp.float32)
        hidden = (gate_part / (1.0 + jnp.exp(-gate_part)) * up_part).astype(result.dtype)

        @pl.when(g > 0)
        def _():
            loop(jnp.maximum(first - group, 1), first, add_and_send)

        forward_piece(1)
        for piece in range(2):
            columns = slice(piece * (width // 2), (piece + 1) * (width // 2))
            y = jnp.dot(hidden, down_w[:, columns], preferred_element_type=jnp.float32)
            result[pl.ds(first, group), :, :, columns] = y.astype(result.dtype).reshape(
                group, 2, most, width // 2
            )
            forward_piece(2 + piece)
        loop(first, first + group, lambda k: across(k).start())

    loop(0, groups, step)
    loop(at.pairs - group, at.pairs, add_and_send)
    add(0)
    keep = pltpu.make_async_copy(part.at[0], out_ref.at[at.pair], keep_sem.at[0])
    keep.start()

    def settle(k):
        pair = source(k)
        pltpu.make_async_remote_copy(
            src_ref=part.at[k],
            dst_ref=out_ref.at[pair],
            send_sem=home_sem.at[k],
            recv_sem=done_sem.at[pair],
            device_id=at.partner,
            device_id_type=MESH,
        ).wait_recv()

    loop(1, at.pairs, settle)
    keep.wait()
    own.wait_send()
    across(0).wait_send()

    def drain(k):
        outward(k).wait_send()
        sideways(k, at.odd).wait_send()
        across(k).wait_send()
        home(k).wait_send()

    loop(1, at.pairs, drain)


def experts_layer(x, w_gate, w_up, w_down, replicas, count):
    pairs, most, width = x.shape
    group = min(pairs // 2, max(PIECES, 64 // most))
    hidden_units = w_gate.shape[1]
    weight = pltpu.VMEM((hidden_units, width), w_gate.dtype)
    return pl.pallas_call(
        functools.partial(experts_kernel, replicas, count, group),
        out_shape=jax.ShapeDtypeStruct(x.shape, x.dtype),
        in_specs=[pl.BlockSpec(memory_space=pltpu.VMEM)] + [pl.BlockSpec(memory_space=pl.ANY)] * 3,
        out_specs=pl.BlockSpec(memory_space=pl.ANY),
        scratch_shapes=[
            weight,
            weight,
            weight,
            pltpu.VMEM((pairs, 2, most, width), x.dtype),
            pltpu.VMEM((pairs, 2, most, width), x.dtype),
            pltpu.VMEM((pairs, most, width), x.dtype),
            pltpu.SemaphoreType.DMA((3,)),
            pltpu.SemaphoreType.DMA((pairs,)),
            pltpu.SemaphoreType.DMA((pairs,)),
            pltpu.SemaphoreType.DMA((pairs, 2)),
            pltpu.SemaphoreType.DMA((pairs,)),
            pltpu.SemaphoreType.DMA((pairs,)),
            pltpu.SemaphoreType.DMA((pairs,)),
            pltpu.SemaphoreType.DMA((pairs,)),
            pltpu.SemaphoreType.DMA((1,)),
        ],
        compiler_params=pltpu.CompilerParams(
            collective_id=1, has_side_effects=True, vmem_limit_bytes=56 * 1024 * 1024
        ),
    )(x, w_gate, w_up, w_down)


def on_device(
    head_outputs, out_weight, residual, norm_gain, chosen, gates, place, w_gate, w_up, w_down
):
    tensor_count = lax.axis_size("tensor")
    replica_count = lax.axis_size("dp")
    owners = replica_count * tensor_count
    my_index = lax.axis_index("dp") * tensor_count + lax.axis_index("tensor")
    row_count = residual.shape[0]
    model_width = residual.shape[1]
    projected = project(head_outputs, out_weight, tensor_count)
    layer_state = residual.astype(jnp.float32) + projected
    scale = lax.rsqrt(jnp.mean(layer_state * layer_state, axis=1, keepdims=True) + 1.0)
    normed = (layer_state * scale * norm_gain[None, :]).astype(jnp.bfloat16)
    experts = place.shape[0]
    capacity = chosen.shape[1]
    most = 2 * capacity // owners
    pair_map = (place[None, :] == jnp.arange(experts, dtype=jnp.int32)[:, None]).astype(jnp.float32)
    chosen_pair = jnp.dot(
        pair_map, chosen.astype(jnp.float32), precision=lax.Precision.HIGHEST
    ).astype(jnp.int32)
    gates_pair = jnp.dot(pair_map, gates, precision=lax.Precision.HIGHEST)
    local_row = chosen_pair - my_index * row_count
    is_mine = (local_row >= 0) & (local_row < row_count)
    mine_float = is_mine.astype(jnp.float32)
    capacity_ids = jnp.arange(capacity, dtype=jnp.int32)
    earlier = (capacity_ids[:, None] < capacity_ids[None, :]).astype(jnp.float32)
    slot_rank = jnp.dot(mine_float, earlier, precision=lax.Precision.HIGHEST).astype(jnp.int32)
    matches = is_mine[:, :, None] & (
        slot_rank[:, :, None] == jnp.arange(most, dtype=jnp.int32)[None, None, :]
    )
    match_count = matches.astype(jnp.int32)
    send_row = jnp.sum(match_count * local_row[:, :, None], axis=1)
    send_valid = jnp.sum(match_count, axis=1) > 0
    send_gate = jnp.sum(jnp.where(matches, gates_pair[:, :, None], 0.0), axis=1)
    targets = send_row.reshape(-1)
    valid_flat = send_valid.reshape(-1)
    row_ids = jnp.arange(row_count, dtype=jnp.int32)
    selector = ((targets[:, None] == row_ids[None, :]) & valid_flat[:, None]).astype(jnp.bfloat16)
    picked = jnp.dot(selector, normed, preferred_element_type=jnp.float32).astype(jnp.bfloat16)
    picked = picked.reshape(experts, most, model_width)
    returned = experts_layer(picked, w_gate, w_up, w_down, replica_count, tensor_count)
    summed = returned.reshape(experts * most, model_width).astype(jnp.float32)
    combine = jnp.where(
        (targets[None, :] == row_ids[:, None]) & valid_flat[None, :],
        send_gate.reshape(-1)[None, :],
        0.0,
    )
    moe = jnp.dot(combine, summed, precision=lax.Precision.HIGHEST)
    return (layer_state + moe).astype(jnp.bfloat16)


def solution(mesh):
    return jax.shard_map(
        on_device,
        mesh=mesh,
        in_specs=(
            P("dp", "tensor"),
            P("tensor", None),
            P(("dp", "tensor"), None),
            P(),
            P(),
            P(),
            P(),
            P(("dp", "tensor"), None, None),
            P(("dp", "tensor"), None, None),
            P(("dp", "tensor"), None, None),
        ),
        out_specs=P(("dp", "tensor"), None),
        check_vma=False,
    )
```

profile of v0, /device:TPU:1, one launch (start us, length us, event | category | flops | bytes accessed | tf_op | source)
XLA Modules:
  0.0 218.2 jit_solution(3436741195735199007)
XLA Ops:
  0.0 0.0 copy-start
  0.0 0.7 copy-done
  0.7 0.8 fusion.17
  1.5 0.9 compare_and_fusion
  2.4 0.2 convolution_convert_fusion.1
  2.5 0.1 select_reduce_fusion
  2.7 0.6 convert_reduce_fusion
  3.3 0.1 broadcast_in_dim.24
  3.4 0.1 gt.19
  3.5 0.1 eq.60
  3.6 0.0 copy-start.1
  3.6 1.2 copy-done.1
  4.8 0.0 copy-start.2
  4.8 85.4 %shard_map.100 = f32[128,4096]{1,0:T(8,128)S(1)} custom-call(bf16[1024,512]{1,0:T(8,128)(2,1)S(1)} %copy-done.1, bf16[512,4096]{1,0:T(8,128)(2,1)} %w_ref.1), custom_call_target="tpu_custom_call" | custom-call | tf_op jit(solution)/shard_map/pallas_call | solution.py:104
  90.2 0.0 copy-done.2
  90.3 0.0 copy-start.3
  90.3 0.4 multiply_reduce_fusion
  90.7 0.3 copy-done.3
  91.0 2.1 convolution_convert_fusion
  93.1 121.3 %shard_map.101 = bf16[16,16,4096]{2,1,0:T(8,128)(2,1)} custom-call(bf16[16,16,4096]{2,1,0:T(8,128)(2,1)} %bitcast.5, bf16[1,704,4096]{2,1,0:T(8,128)(2,1)} %gate_hbm.1, bf16[1,704,4096]{2,1,0:T(8,128)(2,1)} %up_hbm.1, bf16[1,704,4096]{2,1,0:T(8,128)(2,1)} %down_hbm.1), custom_call_target="tpu_custom_call" | custom-call | tf_op jit(solution)/shard_map/pallas_call | solution.py:336
  214.5 3.7 %fusion = bf16[128,4096]{1,0:T(8,128)(2,1)} fusion(bf16[256,4096]{1,0:T(8,128)(2,1)} %bitcast.6, f32[128,4096]{1,0:T(8,128)S(1)} %shard_map.100, bf16[128,4096]{1,0:T(8,128)(2,1)S(1)} %copy-done.2, f32[256]{0:T(256)S(1)} %broadcast_in_dim.24, s32[256]{0:T(256)S(1)} %eq.60, pred[256]{0:T(512)(128)(4,1)S(1)} %gt.19), kind=kOutput, calls=%fused_computation.2 | convolution fusion | flops 1612808192 | bytes 6293760 | tf_op jit(solution)/shard_map/dot_general | solution.py:411
  (2 shorter events, 0.0 us)
Async XLA Ops:
  0.0 0.7 copy-start
  3.6 1.2 copy-start.1
  4.8 85.4 %copy-start.2 = (bf16[128,4096]{1,0:T(8,128)(2,1)S(1)}, bf16[128,4096]{1,0:T(8,128)(2,1)}, u32[]{:S(2)}) copy-start(bf16[128,4096]{1,0:T(8,128)(2,1)} %param.12) | copy-start | bytes 3145732
  90.3 0.7 copy-start.3
where the time goes:
time: 219 us; the launch traced here: 218 us
  Pallas kernels  207 us (95%)
  matrix products  7.63 us (3%)
  local copies, waits for them, and re-layouts  2.53 us (1%)
    pallas_call x1, Pallas kernels, experts_layer(): pl.pallas_call(functools.partial(experts_kernel, replicas, count, group),...  121 us
    pallas_call x1, Pallas kernels, project(): pl.pallas_call(functools.partial(project_kernel, count), out_shape=jax.Sh...  85.4 us

commit v1 on v0

v1 whole, which is shorter than its diff:
```python
import functools

import jax
import jax.numpy as jnp
from jax import lax
from jax.experimental import pallas as pl
from jax.experimental.pallas import tpu as pltpu
from jax.sharding import PartitionSpec as P

MESH = pl.DeviceIdType.MESH
LANES = 4
PIECES = 4
SEND_ORDER = (1, 2, 3, 0)
FORWARD_ORDER = (0, 2, 1, 3)
COMPUTE_ORDER = (2, 0, 3, 1)
EARLY = 2


def ring_rank(position, count):
    upper = position // (count // 2)
    return (1 - upper) * 2 * position + upper * (2 * (count - 1 - position) + 1)


def routing(place, chosen, gates, my_index, row_count, pick, gain_ref):
    experts, capacity = chosen.shape
    most = pick.shape[1]
    pair_ids = lax.broadcasted_iota(jnp.int32, (experts, experts), 0)
    pair_map = (place == pair_ids).astype(jnp.float32)
    chosen_pair = jnp.dot(
        pair_map,
        chosen.astype(jnp.float32),
        precision=lax.Precision.HIGHEST,
        preferred_element_type=jnp.float32,
    ).astype(jnp.int32)
    gates_pair = jnp.dot(
        pair_map, gates, precision=lax.Precision.HIGHEST, preferred_element_type=jnp.float32
    )
    local_row = chosen_pair - my_index * row_count
    is_mine = (local_row >= 0) & (local_row < row_count)
    before = lax.broadcasted_iota(jnp.int32, (capacity, capacity), 0)
    after = lax.broadcasted_iota(jnp.int32, (capacity, capacity), 1)
    slot_rank = jnp.dot(
        is_mine.astype(jnp.float32).astype(jnp.bfloat16),
        (before < after).astype(jnp.float32).astype(jnp.bfloat16),
        preferred_element_type=jnp.float32,
    ).astype(jnp.int32)
    row_ids = lax.broadcasted_iota(jnp.int32, (experts, row_count), 1)
    shifted = (local_row + 1).astype(jnp.float32)
    for m in range(most):
        match = is_mine & (slot_rank == m)
        target = jnp.sum(jnp.where(match, shifted, 0.0), axis=1, keepdims=True)
        gate = jnp.sum(jnp.where(match, gates_pair, 0.0), axis=1, keepdims=True)
        hit = target.astype(jnp.int32) - 1 == row_ids
        pick[:, m, :] = hit.astype(jnp.float32)
        gain_ref[:, m, :] = jnp.where(hit, gate, 0.0)


def project_kernel(
    replicas,
    count,
    x_hbm,
    w_hbm,
    residual_ref,
    norm_ref,
    chosen_ref,
    gates_ref,
    place_ref,
    state_ref,
    picked_ref,
    combine_ref,
    x_ref,
    w_ref,
    held,
    term,
    pick,
    load_sem,
    send_sem,
    recv_sem,
):
    dp = lax.axis_index("dp")
    rank = lax.axis_index("tensor")
    odd = rank % 2
    half = rank // 2
    here = (1 - odd) * half + odd * (count - 1 - half)
    right = ring_rank((here + 1) % count, count)
    left = ring_rank((here + count - 1) % count, count)
    rows = state_ref.shape[0]
    width = state_ref.shape[1] // LANES
    order = [lane for k in range(LANES // 2) for lane in (k, LANES // 2 + k)]

    def columns(lane):
        return slice(lane * width, (lane + 1) * width)

    loads = {
        lane: pltpu.make_async_copy(
            w_hbm.at[:, columns(lane)], w_ref.at[:, columns(lane)], load_sem.at[lane]
        )
        for lane in order
    }
    x_load = pltpu.make_async_copy(x_hbm, x_ref, load_sem.at[LANES])
    loads[order[0]].start()
    x_load.start()
    for lane in order[1:]:
        loads[lane].start()

    def own_term(lane, block):
        start = pl.multiple_of(ring_rank(block, count) * rows, rows)
        return jnp.dot(
            x_ref[pl.ds(start, rows), :],
            w_ref[:, columns(lane)],
            preferred_element_type=jnp.float32,
        )

    def block_of(lane, slot):
        if lane < LANES // 2:
            return (here + 2 * count - 1 - slot) % count
        return (here + 1 + slot) % count

    def copy(lane, slot):
        return pltpu.make_async_remote_copy(
            src_ref=held.at[lane, slot],
            dst_ref=held.at[lane, slot + 1],
            send_sem=send_sem.at[lane, slot],
            recv_sem=recv_sem.at[lane, slot + 1],
            device_id=(dp, right if lane < LANES // 2 else left),
            device_id_type=MESH,
        )

    def arrival(lane, slot):
        return pltpu.make_async_remote_copy(
            src_ref=held.at[lane, slot],
            dst_ref=held.at[lane, slot],
            send_sem=send_sem.at[lane, slot],
            recv_sem=recv_sem.at[lane, slot],
            device_id=(dp, right if lane < LANES // 2 else left),
            device_id_type=MESH,
        )

    barrier = pltpu.get_barrier_semaphore()
    for neighbour in (left, right):
        pl.semaphore_signal(barrier, inc=1, device_id=(dp, neighbour), device_id_type=MESH)
    x_load.wait()
    for n, lane in enumerate(order):
        loads[lane].wait()
        held[lane, 0] = own_term(lane, block_of(lane, 0)).astype(held.dtype)
        if n == 0:
            pl.semaphore_wait(barrier, 2)
        copy(lane, 0).start()

    routing(
        place_ref[...],
        chosen_ref[...],
        gates_ref[...],
        dp * count + rank,
        rows,
        pick,
        combine_ref,
    )

    def step(slot, carry):
        for lane in order:
            term[lane] = own_term(lane, block_of(lane, slot))
        for lane in order:
            arrival(lane, slot).wait_recv()
            held[lane, slot] = (held[lane, slot].astype(jnp.float32) + term[lane]).astype(held.dtype)
            copy(lane, slot).start()
        return carry

    lax.fori_loop(1, count - 1, step, 0)
    last = count - 1
    for lane in order:
        term[lane] = own_term(lane, block_of(lane, last)) + residual_ref[:, columns(lane)].astype(
            jnp.float32
        )
    total = jnp.zeros((rows, 1), jnp.float32)
    for lane in order:
        arrival(lane, last).wait_recv()
        state = held[lane, last].astype(jnp.float32) + term[lane]
        state_ref[:, columns(lane)] = state
        total = total + jnp.sum(state * state, axis=1, keepdims=True)
    scale = lax.rsqrt(total / (LANES * width) + 1.0)
    selector = pick[...].reshape(picked_ref.shape[0], rows).astype(jnp.bfloat16)
    for lane in order:
        normed = (state_ref[:, columns(lane)] * scale * norm_ref[:, columns(lane)]).astype(
            jnp.bfloat16
        )
        picked_ref[:, columns(lane)] = jnp.dot(
            selector, normed, preferred_element_type=jnp.float32
        ).astype(picked_ref.dtype)

    def drain(slot, carry):
        for lane in order:
            copy(lane, slot).wait_send()
        return carry

    lax.fori_loop(0, count - 1, drain, 0)


def project(x, w, residual, norm_gain, chosen, gates, place, replicas, count):
    rows, columns = residual.shape
    width = columns // LANES
    experts, capacity = chosen.shape
    most = 2 * capacity // (replicas * count)
    whole = pl.BlockSpec(memory_space=pltpu.VMEM)
    outside = pl.BlockSpec(memory_space=pl.ANY)
    return pl.pallas_call(
        functools.partial(project_kernel, replicas, count),
        out_shape=(
            jax.ShapeDtypeStruct((rows, columns), jnp.float32),
            jax.ShapeDtypeStruct((experts * most, columns), jnp.bfloat16),
            jax.ShapeDtypeStruct((experts, most, rows), jnp.float32),
        ),
        in_specs=[outside, outside] + [whole] * 5,
        out_specs=(whole, whole, whole),
        scratch_shapes=[
            pltpu.VMEM(x.shape, x.dtype),
            pltpu.VMEM(w.shape, w.dtype),
            pltpu.VMEM((LANES, count, rows, width), jnp.bfloat16),
            pltpu.VMEM((LANES, rows, width), jnp.float32),
            pltpu.VMEM((experts, most, rows), jnp.float32),
            pltpu.SemaphoreType.DMA((LANES + 1,)),
            pltpu.SemaphoreType.DMA((LANES, count)),
            pltpu.SemaphoreType.DMA((LANES, count)),
        ],
        compiler_params=pltpu.CompilerParams(
            collective_id=0, has_side_effects=True, vmem_limit_bytes=60 * 1024 * 1024
        ),
    )(x, w, residual, norm_gain[None, :], chosen, gates, place[None, :])


class Place:
    def __init__(self, replicas, count):
        self.dp = lax.axis_index("dp")
        rank = lax.axis_index("tensor")
        self.odd = rank % 2
        self.per_row = count // 2
        self.pairs = replicas * self.per_row
        self.pair = self.dp * self.per_row + rank // 2
        self.partner = (self.dp, rank + 1 - 2 * self.odd)

    def device(self, pair):
        return (pair // self.per_row, 2 * (pair % self.per_row) + self.odd)

    def toggle(self, number):
        replicas = self.pairs // self.per_row
        other = (number % replicas) * self.per_row + number // replicas
        total = 0
        bit = 1
        while bit < self.pairs:
            total = total + ((self.pair // bit + other // bit) % 2) * bit
            bit *= 2
        return total

    def greet(self):
        barrier = pltpu.get_barrier_semaphore()

        def signal(k, carry):
            target = self.device((self.pair + k) % self.pairs)
            pl.semaphore_signal(barrier, inc=1, device_id=target, device_id_type=MESH)
            return carry

        lax.fori_loop(1, self.pairs, signal, 0)
        pl.semaphore_signal(barrier, inc=1, device_id=self.partner, device_id_type=MESH)
        pl.semaphore_wait(barrier, self.pairs)


def loop(start, stop, body):
    def step(k, carry):
        body(k)
        return carry

    lax.fori_loop(start, stop, step, 0)


def experts_kernel(
    replicas,
    count,
    group,
    x_ref,
    state_ref,
    combine_ref,
    gate_hbm,
    up_hbm,
    down_hbm,
    out_ref,
    gate_w,
    up_w,
    down_w,
    received,
    result,
    part,
    returned,
    weight_sem,
    send_sem,
    pass_sem,
    recv_sem,
    cross_sem,
    part_sem,
    home_sem,
    done_sem,
):
    at = Place(replicas, count)
    most, width = x_ref.shape[1:]
    rows = group * 2 * most
    groups = at.pairs // group

    def source(k):
        return at.toggle(k)

    def outward(k):
        target = at.toggle(k)
        return pltpu.make_async_remote_copy(
            src_ref=x_ref.at[target],
            dst_ref=received.at[k, at.odd],
            send_sem=send_sem.at[k],
            recv_sem=recv_sem.at[k, at.odd],
            device_id=at.device(target),
            device_id_type=MESH,
        )

    def sideways(k, side):
        return pltpu.make_async_remote_copy(
            src_ref=received.at[k, side],
            dst_ref=received.at[k, side],
            send_sem=pass_sem.at[k],
            recv_sem=recv_sem.at[k, side],
            device_id=at.partner,
            device_id_type=MESH,
        )

    def across(k):
        return pltpu.make_async_remote_copy(
            src_ref=result.at[k, 1 - at.odd],
            dst_ref=part.at[k],
            send_sem=cross_sem.at[k],
            recv_sem=part_sem.at[k],
            device_id=at.partner,
            device_id_type=MESH,
        )

    def home(k):
        return pltpu.make_async_remote_copy(
            src_ref=part.at[k],
            dst_ref=returned.at[at.pair],
            send_sem=home_sem.at[k],
            recv_sem=done_sem.at[at.pair],
            device_id=at.device(source(k)),
            device_id_type=MESH,
        )

    def forward(k):
        sideways(k, at.odd).wait_recv()
        sideways(k, at.odd).start()

    def add(k):
        across(k).wait_recv()
        part[k] = (
            part[k].astype(jnp.float32) + result[k, at.odd].astype(jnp.float32)
        ).astype(part.dtype)

    def add_and_send(k):
        add(k)
        home(k).start()

    loads = [
        pltpu.make_async_copy(hbm.at[0], vmem, weight_sem.at[n])
        for n, (hbm, vmem) in enumerate(((gate_hbm, gate_w), (up_hbm, up_w), (down_hbm, down_w)))
    ]
    for load in loads:
        load.start()
    own = pltpu.make_async_remote_copy(
        src_ref=x_ref.at[at.pair],
        dst_ref=received.at[0, at.odd],
        send_sem=pass_sem.at[0],
        recv_sem=recv_sem.at[0, at.odd],
        device_id=at.partner,
        device_id_type=MESH,
    )
    at.greet()

    def members(g):
        return max(g * group, 1), (g + 1) * group

    for g in SEND_ORDER:
        loop(*members(g), lambda k: outward(k).start())
    own.start()
    received[0, at.odd] = x_ref[at.pair]
    for g in FORWARD_ORDER[:EARLY]:
        loop(*members(g), forward)
    for load in loads:
        load.wait()
    contract = (((1,), (1,)), ((), ()))
    late = FORWARD_ORDER[EARLY:]

    def code_of(numbers):
        return sum(number * groups**n for n, number in enumerate(numbers))

    def step(i, carry):
        compute_code, forward_code, before = carry
        first = (compute_code % groups) * group
        start = (forward_code % groups) * group

        def forward_piece(piece):
            @pl.when(i < len(late))
            def _():
                cut = [start + n * group // PIECES for n in (piece, piece + 1)]
                loop(jnp.maximum(cut[0], 1), cut[1], forward)

        loop(first, first + group, lambda k: sideways(k, 1 - at.odd).wait_recv())
        x = received[pl.ds(first, group)].reshape(rows, width)
        gate_part = lax.dot_general(x, gate_w[...], contract, preferred_element_type=jnp.float32)
        forward_piece(0)
        up_part = lax.dot_general(x, up_w[...], contract, preferred_element_type=jnp.float32)
        hidden = (gate_part / (1.0 + jnp.exp(-gate_part)) * up_part).astype(result.dtype)

        @pl.when(i > 0)
        def _():
            loop(jnp.maximum(before, 1), before + group, add_and_send)

        forward_piece(1)
        for piece in range(2):
            columns = slice(piece * (width // 2), (piece + 1) * (width // 2))
            y = jnp.dot(hidden, down_w[:, columns], preferred_element_type=jnp.float32)
            result[pl.ds(first, group), :, :, columns] = y.astype(result.dtype).reshape(
                group, 2, most, width // 2
            )
            forward_piece(2 + piece)
        loop(first, first + group, lambda k: across(k).start())
        return compute_code // groups, forward_code // groups, first

    lax.fori_loop(0, groups, step, (code_of(COMPUTE_ORDER), code_of(late), 0))
    loop(*members(COMPUTE_ORDER[-1]), add_and_send)
    add(0)
    returned[at.pair] = part[0]

    def settle(k):
        pair = source(k)
        pltpu.make_async_remote_copy(
            src_ref=part.at[k],
            dst_ref=returned.at[pair],
            send_sem=home_sem.at[k],
            recv_sem=done_sem.at[pair],
            device_id=at.partner,
            device_id_type=MESH,
        ).wait_recv()

    loop(1, at.pairs, settle)
    combine = combine_ref[...].reshape(at.pairs * most, state_ref.shape[0])
    coarse = combine.astype(jnp.bfloat16)
    fine = (combine - coarse.astype(jnp.float32)).astype(jnp.bfloat16)
    over_slots = (((0,), (0,)), ((), ()))
    for piece in range(PIECES):
        columns = slice(piece * (width // PIECES), (piece + 1) * (width // PIECES))
        slots = returned[:, :, columns].reshape(at.pairs * most, width // PIECES)
        moe = lax.dot_general(
            coarse, slots, over_slots, preferred_element_type=jnp.float32
        ) + lax.dot_general(fine, slots, over_slots, preferred_element_type=jnp.float32)
        out_ref[:, columns] = (state_ref[:, columns] + moe).astype(out_ref.dtype)
    own.wait_send()
    across(0).wait_send()

    def drain(k):
        outward(k).wait_send()
        sideways(k, at.odd).wait_send()
        across(k).wait_send()
        home(k).wait_send()

    loop(1, at.pairs, drain)


def experts_layer(x, state, combine, w_gate, w_up, w_down, replicas, count):
    pairs, most, width = x.shape
    group = pairs // len(COMPUTE_ORDER)
    hidden_units = w_gate.shape[1]
    weight = pltpu.VMEM((hidden_units, width), w_gate.dtype)
    slots = pltpu.VMEM((pairs, most, width), x.dtype)
    sides = pltpu.VMEM((pairs, 2, most, width), x.dtype)
    whole = pl.BlockSpec(memory_space=pltpu.VMEM)
    return pl.pallas_call(
        functools.partial(experts_kernel, replicas, count, group),
        out_shape=jax.ShapeDtypeStruct(state.shape, x.dtype),
        in_specs=[whole] * 3 + [pl.BlockSpec(memory_space=pl.ANY)] * 3,
        out_specs=whole,
        scratch_shapes=[
            weight,
            weight,
            weight,
            sides,
            sides,
            slots,
            slots,
            pltpu.SemaphoreType.DMA((3,)),
            pltpu.SemaphoreType.DMA((pairs,)),
            pltpu.SemaphoreType.DMA((pairs,)),
            pltpu.SemaphoreType.DMA((pairs, 2)),
            pltpu.SemaphoreType.DMA((pairs,)),
            pltpu.SemaphoreType.DMA((pairs,)),
            pltpu.SemaphoreType.DMA((pairs,)),
            pltpu.SemaphoreType.DMA((pairs,)),
        ],
        compiler_params=pltpu.CompilerParams(
            collective_id=1, has_side_effects=True, vmem_limit_bytes=60 * 1024 * 1024
        ),
    )(x, state, combine, w_gate, w_up, w_down)


def on_device(
    head_outputs, out_weight, residual, norm_gain, chosen, gates, place, w_gate, w_up, w_down
):
    count = lax.axis_size("tensor")
    replicas = lax.axis_size("dp")
    state, picked, combine = project(
        head_outputs, out_weight, residual, norm_gain, chosen, gates, place, replicas, count
    )
    experts, most = combine.shape[:2]
    picked = picked.reshape(experts, most, residual.shape[1])
    return experts_layer(picked, state, combine, w_gate, w_up, w_down, replicas, count)


def solution(mesh):
    return jax.shard_map(
        on_device,
        mesh=mesh,
        in_specs=(
            P("dp", "tensor"),
            P("tensor", None),
            P(("dp", "tensor"), None),
            P(),
            P(),
            P(),
            P(),
            P(("dp", "tensor"), None, None),
            P(("dp", "tensor"), None, None),
            P(("dp", "tensor"), None, None),
        ),
        out_specs=P(("dp", "tensor"), None),
        check_vma=False,
    )
```

time: 219 us -> 212 us (0.968)
  matrix products: 7.63 us -> 0 us
  Pallas kernels: 207 us -> 210 us
    dot_general x5 -> x0, matrix products: 7.63 us -> none  [the longest x1 3.67 us: on_device(): moe = jnp.dot(combine, summed, precision=lax.Precision.HIGHEST)]
    pallas_call x1, Pallas kernels: 85.4 us -> 88.1 us  [project(): pl.pallas_call(functools.partial(project_kernel, replicas, count), out_sh...]
where the time goes in v1:
time: 212 us
  Pallas kernels  210 us (99%)
  local copies, waits for them, and re-layouts  2.29 us (1%)
    pallas_call x1, Pallas kernels, experts_layer(): pl.pallas_call(functools.partial(experts_kernel, replicas, count, group),...  121 us
    pallas_call x1, Pallas kernels, project(): pl.pallas_call(functools.partial(project_kernel, replicas, count), out_sh...  88.1 us

profile of v1, /device:TPU:1, one launch (start us, length us, event | category | flops | bytes accessed | tf_op | source)
XLA Modules:
  0.0 211.8 jit_solution(5891903466335994775)
XLA Ops:
  0.0 88.1 %shard_map.100 = (f32[128,4096]{1,0:T(8,128)}, bf16[256,4096]{1,0:T(8,128)(2,1)}, f32[16,16,128]{2,1,0:T(8,128)}) custom-call(bf16[1024,512]{1,0:T(8,128)(2,1)} %x_hbm.1, bf16[512,4096]{1,0:T(8,128)(2,1)} %w_hbm.1, bf16[128,4096]{1,0:T(8,128)(2,1)} %residual_ref.1, f32[1,4096]{1,0:T(1,128)} %bitcast.4, s32[16,256]{1,0:T(8,128)} %chosen_ref.1, ...), custom_call_target="tpu_custom_call" | custom-call | tf_op jit(solution)/shard_map/pallas_call | solution.py:206
  88.1 121.4 %shard_map.101 = bf16[128,4096]{1,0:T(8,128)(2,1)} custom-call(bf16[16,16,4096]{2,1,0:T(8,128)(2,1)} %bitcast.3, f32[128,4096]{1,0:T(8,128)} %get-tuple-element.9.state_ref, f32[16,16,128]{2,1,0:T(8,128)} %get-tuple-element.10.combine_ref, bf16[1,704,4096]{2,1,0:T(8,128)(2,1)} %gate_hbm.1, bf16[1,704,4096]{2,1,0:T(8,128)(2,1)} %up_hbm.1, ...), custom_call_target="tpu_custom_call" | custom-call | tf_op jit(solution)/shard_map/pallas_call | solution.py:479
  209.5 2.3 %copy.12 = bf16[128,4096]{1,0:T(8,128)(2,1)} copy(bf16[128,4096]{1,0:T(8,128)(2,1)} %shard_map.101) | data formatting | bytes 2097152

commit v2 on v1

--- a/solution.py
+++ b/solution.py
@@ -10,10 +10,11 @@
 MESH = pl.DeviceIdType.MESH
 LANES = 4
 PIECES = 4
+GROUPS = 4
+AHEAD = 2
 SEND_ORDER = (1, 2, 3, 0)
-FORWARD_ORDER = (0, 2, 1, 3)
-COMPUTE_ORDER = (2, 0, 3, 1)
-EARLY = 2
+HOME_ORDER = (2, 3, 1, 0)
+ISSUE = ((2, (2,)), (3, (3, 1, 0)))
 
 
 def ring_rank(position, count):
@@ -223,7 +224,293 @@
             pltpu.SemaphoreType.DMA((LANES, count)),
         ],
         compiler_params=pltpu.CompilerParams(
-            collective_id=0, has_side_effects=True, vmem_limit_bytes=60 * 1024 * 1024
+            collective_id=0, has_side_effects=True, vmem_limit_bytes=44 * 1024 * 1024
+        ),
+    )(x, w, residual, norm_gain[None, :], chosen, gates, place[None, :])
+
+
+def flip(value, bit):
+    return value + bit - 2 * bit * ((value // bit) % 2)
+
+
+def toggled(value, mask):
+    bit = 1
+    while bit <= mask:
+        if mask & bit:
+            value = flip(value, bit)
+        bit *= 2
+    return value
+
+
+def exchange_kernel(
+    replicas,
+    x_hbm,
+    w_hbm,
+    residual_ref,
+    norm_ref,
+    chosen_ref,
+    gates_ref,
+    place_ref,
+    state_ref,
+    picked_ref,
+    combine_ref,
+    lhs,
+    rhs,
+    side_out,
+    side_in,
+    far_out,
+    far_in,
+    pick,
+    load_sem,
+    rows_send,
+    rows_recv,
+    cols_send,
+    cols_recv,
+    relay_sem,
+    side_send,
+    side_recv,
+    far_send,
+    far_recv,
+):
+    dp = lax.axis_index("dp")
+    rank = lax.axis_index("tensor")
+    near, side, far = flip(rank, 2), flip(rank, 1), flip(rank, 4)
+    rows, total = state_ref.shape
+    depth = x_hbm.shape[1]
+    share = total // replicas
+    width = share // PIECES
+    bits = [1 << n for n in range(replicas.bit_length() - 1)]
+    blocks = [(n, 1 - n // 2, n % 2) for n in range(4)]
+
+    def place_of(owner, other_side, other_far):
+        mask = other_side + 4 * other_far
+        return pl.multiple_of(toggled(owner, mask) * rows, rows)
+
+    def cols(origin, piece):
+        return pl.ds(pl.multiple_of(origin * share + piece * width, width), width)
+
+    def rows_copy(n, other_side, other_far):
+        return pltpu.make_async_remote_copy(
+            src_ref=x_hbm.at[pl.ds(place_of(near, other_side, other_far), rows), :],
+            dst_ref=lhs.at[n * rows : (n + 1) * rows, depth:],
+            send_sem=rows_send.at[n],
+            recv_sem=rows_recv.at[n],
+            device_id=(dp, near),
+            device_id_type=MESH,
+        )
+
+    def cols_copy(piece):
+        return pltpu.make_async_remote_copy(
+            src_ref=w_hbm.at[:, cols(dp, piece)],
+            dst_ref=rhs.at[depth:, cols(dp, piece)],
+            send_sem=cols_send.at[piece],
+            recv_sem=cols_recv.at[piece, 0],
+            device_id=(dp, near),
+            device_id_type=MESH,
+        )
+
+    def relay(piece, origin, bit):
+        window = rhs.at[depth:, cols(toggled(dp, origin), piece)]
+        return pltpu.make_async_remote_copy(
+            src_ref=window,
+            dst_ref=window,
+            send_sem=relay_sem.at[piece, origin, bits.index(bit)],
+            recv_sem=cols_recv.at[piece, origin ^ bit],
+            device_id=(flip(dp, bit), rank),
+            device_id_type=MESH,
+        )
+
+    def cols_arrival(piece, origin):
+        window = rhs.at[depth:, cols(toggled(dp, origin), piece)]
+        return pltpu.make_async_remote_copy(
+            src_ref=window,
+            dst_ref=window,
+            send_sem=cols_send.at[piece],
+            recv_sem=cols_recv.at[piece, origin],
+            device_id=(dp, near),
+            device_id_type=MESH,
+        )
+
+    def onward(origin):
+        return [bit for bit in bits if origin % (2 * bit) == 0]
+
+    def side_copy(piece, origin):
+        n = piece * replicas + origin
+        return pltpu.make_async_remote_copy(
+            src_ref=side_out.at[n],
+            dst_ref=side_in.at[n],
+            send_sem=side_send.at[n],
+            recv_sem=side_recv.at[n],
+            device_id=(dp, side),
+            device_id_type=MESH,
+        )
+
+    def far_copy(piece, origin):
+        n = piece * replicas + origin
+        return pltpu.make_async_remote_copy(
+            src_ref=far_out.at[n],
+            dst_ref=far_in.at[n],
+            send_sem=far_send.at[n],
+            recv_sem=far_recv.at[n],
+            device_id=(dp, far),
+            device_id_type=MESH,
+        )
+
+    w_load = pltpu.make_async_copy(w_hbm, rhs.at[:depth, :], load_sem.at[0])
+    x_loads = [
+        pltpu.make_async_copy(
+            x_hbm.at[pl.ds(place_of(rank, other_side, other_far), rows), :],
+            lhs.at[n * rows : (n + 1) * rows, :depth],
+            load_sem.at[1 + n],
+        )
+        for n, other_side, other_far in blocks
+    ]
+    barrier = pltpu.get_barrier_semaphore()
+    partners = [(dp, near), (dp, side), (dp, far)] + [(flip(dp, bit), rank) for bit in bits]
+    for partner in partners:
+        pl.semaphore_signal(barrier, inc=1, device_id=partner, device_id_type=MESH)
+    w_load.start()
+    for load in x_loads:
+        load.start()
+    pl.semaphore_wait(barrier, len(partners))
+    for block in blocks[:2]:
+        rows_copy(*block).start()
+    cols_copy(0).start()
+    for block in blocks[2:]:
+        rows_copy(*block).start()
+    for piece in range(1, PIECES):
+        cols_copy(piece).start()
+    routing(
+        place_ref[...],
+        chosen_ref[...],
+        gates_ref[...],
+        dp * lax.axis_size("tensor") + rank,
+        rows,
+        pick,
+        combine_ref,
+    )
+    w_load.wait()
+    for load in x_loads:
+        load.wait()
+    for block in blocks[:2]:
+        rows_copy(*block).wait_recv()
+
+    def begin(piece, origin):
+        cols_arrival(piece, origin).wait_recv()
+        for bit in onward(origin):
+            relay(piece, origin, bit).start()
+        here = cols(toggled(dp, origin), piece)
+        side_out[piece * replicas + origin] = jnp.dot(
+            lhs[: 2 * rows, :], rhs[:, here], preferred_element_type=jnp.float32
+        ).astype(side_out.dtype)
+        side_copy(piece, origin).start()
+
+    def middle(piece, origin):
+        n = piece * replicas + origin
+        here = cols(toggled(dp, origin), piece)
+        own = jnp.dot(lhs[2 * rows :, :], rhs[:, here], preferred_element_type=jnp.float32)
+        side_copy(piece, origin).wait_recv()
+        both = own + side_in[n].astype(jnp.float32)
+        far_out[n] = both[rows:].astype(far_out.dtype)
+        far_copy(piece, origin).start()
+        state_ref[:, here] = both[:rows] + residual_ref[:, here].astype(jnp.float32)
+
+    begin(0, 0)
+    begin(0, 1)
+    for block in blocks[2:]:
+        rows_copy(*block).wait_recv()
+
+    def step(piece, carry):
+        for origin in range(replicas):
+            if origin < 2:
+
+                @pl.when(piece > 0)
+                def _():
+                    begin(piece, origin)
+                    middle(piece - 1, origin + replicas - 2)
+
+            else:
+                begin(piece, origin)
+                middle(piece, origin - 2)
+        return carry
+
+    lax.fori_loop(0, PIECES, step, 0)
+    middle(PIECES - 1, replicas - 2)
+    middle(PIECES - 1, replicas - 1)
+
+    def finish(piece, squares):
+        for origin in range(replicas):
+            here = cols(toggled(dp, origin), piece)
+            far_copy(piece, origin).wait_recv()
+            state = state_ref[:, here] + far_in[piece * replicas + origin].astype(jnp.float32)
+            state_ref[:, here] = state
+            squares = squares + jnp.sum(state * state, axis=1, keepdims=True)
+        return squares
+
+    squares = lax.fori_loop(0, PIECES, finish, jnp.zeros((rows, 1), jnp.float32))
+    scale = lax.rsqrt(squares / total + 1.0)
+    selector = pick[...].reshape(picked_ref.shape[0], rows).astype(jnp.bfloat16)
+    for lane in range(LANES):
+        here = slice(lane * (total // LANES), (lane + 1) * (total // LANES))
+        normed = (state_ref[:, here] * scale * norm_ref[:, here]).astype(jnp.bfloat16)
+        picked_ref[:, here] = jnp.dot(
+            selector, normed, preferred_element_type=jnp.float32
+        ).astype(picked_ref.dtype)
+    for block in blocks:
+        rows_copy(*block).wait_send()
+
+    def drain(piece, carry):
+        cols_copy(piece).wait_send()
+        for origin in range(replicas):
+            for bit in onward(origin):
+                relay(piece, origin, bit).wait_send()
+            side_copy(piece, origin).wait_send()
+            far_copy(piece, origin).wait_send()
+        return carry
+
+    lax.fori_loop(0, PIECES, drain, 0)
+
+
+def exchange(x, w, residual, norm_gain, chosen, gates, place, replicas, count):
+    rows, columns = residual.shape
+    depth = x.shape[1]
+    width = columns // replicas // PIECES
+    number = replicas * PIECES
+    experts, capacity = chosen.shape
+    most = 2 * capacity // (replicas * count)
+    whole = pl.BlockSpec(memory_space=pltpu.VMEM)
+    outside = pl.BlockSpec(memory_space=pl.ANY)
+    dma = pltpu.SemaphoreType.DMA
+    return pl.pallas_call(
+        functools.partial(exchange_kernel, replicas),
+        out_shape=(
+            jax.ShapeDtypeStruct((rows, columns), jnp.float32),
+            jax.ShapeDtypeStruct((experts * most, columns), jnp.bfloat16),
+            jax.ShapeDtypeStruct((experts, most, rows), jnp.float32),
+        ),
+        in_specs=[outside, outside] + [whole] * 5,
+        out_specs=(whole, whole, whole),
+        scratch_shapes=[
+            pltpu.VMEM((4 * rows, 2 * depth), x.dtype),
+            pltpu.VMEM((2 * depth, columns), w.dtype),
+            pltpu.VMEM((number, 2 * rows, width), jnp.bfloat16),
+            pltpu.VMEM((number, 2 * rows, width), jnp.bfloat16),
+            pltpu.VMEM((number, rows, width), jnp.bfloat16),
+            pltpu.VMEM((number, rows, width), jnp.bfloat16),
+            pltpu.VMEM((experts, most, rows), jnp.float32),
+            dma((5,)),
+            dma((4,)),
+            dma((4,)),
+            dma((PIECES,)),
+            dma((PIECES, replicas)),
+            dma((PIECES, replicas, replicas.bit_length() - 1)),
+            dma((number,)),
+            dma((number,)),
+            dma((number,)),
+            dma((number,)),
+        ],
+        compiler_params=pltpu.CompilerParams(
+            collective_id=2, has_side_effects=True, vmem_limit_bytes=44 * 1024 * 1024
         ),
     )(x, w, residual, norm_gain[None, :], chosen, gates, place[None, :])
 
@@ -243,7 +530,13 @@
 
     def toggle(self, number):
         replicas = self.pairs // self.per_row
-        other = (number % replicas) * self.per_row + number // replicas
+        near = number // replicas, number % replicas
+        beyond = number - self.pairs // 2
+        steps = self.per_row // 2
+        far = steps + beyond % steps, beyond // steps
+        is_far = number // (self.pairs // 2)
+        row, column = (is_far * b + (1 - is_far) * a for a, b in zip(near, far))
+        other = column * self.per_row + row
         total = 0
         bit = 1
         while bit < self.pairs:
@@ -385,26 +678,21 @@
         loop(*members(g), lambda k: outward(k).start())
     own.start()
     received[0, at.odd] = x_ref[at.pair]
-    for g in FORWARD_ORDER[:EARLY]:
+    for g in range(AHEAD):
         loop(*members(g), forward)
     for load in loads:
         load.wait()
     contract = (((1,), (1,)), ((), ()))
-    late = FORWARD_ORDER[EARLY:]
-
-    def code_of(numbers):
-        return sum(number * groups**n for n, number in enumerate(numbers))
-
-    def step(i, carry):
-        compute_code, forward_code, before = carry
-        first = (compute_code % groups) * group
-        start = (forward_code % groups) * group
+
+    def step(g, carry):
+        first = g * group
+        start = first + AHEAD * group
 
         def forward_piece(piece):
-            @pl.when(i < len(late))
+            @pl.when(g + AHEAD < GROUPS)
             def _():
                 cut = [start + n * group // PIECES for n in (piece, piece + 1)]
-                loop(jnp.maximum(cut[0], 1), cut[1], forward)
+                loop(cut[0], cut[1], forward)
 
         loop(first, first + group, lambda k: sideways(k, 1 - at.odd).wait_recv())
         x = received[pl.ds(first, group)].reshape(rows, width)
@@ -412,11 +700,6 @@
         forward_piece(0)
         up_part = lax.dot_general(x, up_w[...], contract, preferred_element_type=jnp.float32)
         hidden = (gate_part / (1.0 + jnp.exp(-gate_part)) * up_part).astype(result.dtype)
-
-        @pl.when(i > 0)
-        def _():
-            loop(jnp.maximum(before, 1), before + group, add_and_send)
-
         forward_piece(1)
         for piece in range(2):
             columns = slice(piece * (width // 2), (piece + 1) * (width // 2))
@@ -425,11 +708,25 @@
                 group, 2, most, width // 2
             )
             forward_piece(2 + piece)
-        loop(first, first + group, lambda k: across(k).start())
-        return compute_code // groups, forward_code // groups, first
-
-    lax.fori_loop(0, groups, step, (code_of(COMPUTE_ORDER), code_of(late), 0))
-    loop(*members(COMPUTE_ORDER[-1]), add_and_send)
+
+        for n, sets in ISSUE:
+            @pl.when(g == n)
+            def _():
+                for h in sets:
+                    crossing(h)
+
+        return carry
+
+    def crossing(g):
+        loop(0, group, lambda k: across((g + 1) * group - 1 - k).start())
+
+    def homeward(g):
+        low, high = members(g)
+        loop(0, high - low, lambda k: add_and_send(high - 1 - k))
+
+    lax.fori_loop(0, GROUPS, step, 0)
+    for g in HOME_ORDER:
+        homeward(g)
     add(0)
     returned[at.pair] = part[0]
 
@@ -470,7 +767,7 @@
 
 def experts_layer(x, state, combine, w_gate, w_up, w_down, replicas, count):
     pairs, most, width = x.shape
-    group = pairs // len(COMPUTE_ORDER)
+    group = pairs // GROUPS
     hidden_units = w_gate.shape[1]
     weight = pltpu.VMEM((hidden_units, width), w_gate.dtype)
     slots = pltpu.VMEM((pairs, most, width), x.dtype)
@@ -499,7 +796,7 @@
             pltpu.SemaphoreType.DMA((pairs,)),
         ],
         compiler_params=pltpu.CompilerParams(
-            collective_id=1, has_side_effects=True, vmem_limit_bytes=60 * 1024 * 1024
+            collective_id=1, has_side_effects=True, vmem_limit_bytes=44 * 1024 * 1024
         ),
     )(x, state, combine, w_gate, w_up, w_down)
 
@@ -509,7 +806,8 @@
 ):
     count = lax.axis_size("tensor")
     replicas = lax.axis_size("dp")
-    state, picked, combine = project(
+    first = exchange if count == 8 and replicas >= 4 else project
+    state, picked, combine = first(
         head_outputs, out_weight, residual, norm_gain, chosen, gates, place, replicas, count
     )
     experts, most = combine.shape[:2]

time: 212 us -> 198 us (0.934)
  Pallas kernels: 210 us -> 190 us
  local copies, waits for them, and re-layouts: 2.29 us -> 6.23 us
    pallas_call x1, Pallas kernels: 121 us -> 111 us  [experts_layer(): pl.pallas_call(functools.partial(experts_kernel, replicas, count, group),...]
    pallas_call x1, Pallas kernels: 88.1 us -> 79.4 us  [exchange(): pl.pallas_call(functools.partial(exchange_kernel, replicas), out_shape=(j...]
    unnamed x1 -> x13, local copies, waits for them, and re-layouts: 2.29 us -> 6.23 us
where the time goes in v2:
time: 198 us; the launch traced here: 197 us
  Pallas kernels  190 us (96%)
  local copies, waits for them, and re-layouts  6.23 us (3%)
    pallas_call x1, Pallas kernels, experts_layer(): pl.pallas_call(functools.partial(experts_kernel, replicas, count, group),...  111 us
    pallas_call x1, Pallas kernels, exchange(): pl.pallas_call(functools.partial(exchange_kernel, replicas), out_shape=(j...  79.4 us
    unnamed x13, local copies, waits for them, and re-layouts  6.23 us

profile of v2, /device:TPU:1, one launch (start us, length us, event | category | flops | bytes accessed | tf_op | source)
XLA Modules:
  0.0 196.6 jit_solution(13975655135623581681)
XLA Ops:
  0.0 0.0 copy-start
  0.0 1.2 copy-done
  1.2 0.0 copy-start.1
  1.2 1.2 copy-done.1
  2.5 0.0 copy-start.2
  2.5 0.7 copy-done.2
  3.2 0.0 copy-start.3
  3.2 0.7 copy-done.3
  3.9 0.0 copy-start.4
  3.9 0.7 copy-done.4
  4.6 0.0 copy-start.5
  4.6 0.7 copy-done.5
  5.3 79.4 %shard_map.100 = (f32[128,4096]{1,0:T(8,128)S(1)}, bf16[256,4096]{1,0:T(8,128)(2,1)S(1)}, f32[16,16,128]{2,1,0:T(8,128)S(1)}) custom-call(bf16[1024,512]{1,0:T(8,128)(2,1)S(1)} %copy-done, bf16[512,4096]{1,0:T(8,128)(2,1)} %w_hbm.1, bf16[128,4096]{1,0:T(8,128)(2,1)S(1)} %copy-done.1, f32[1,4096]{1,0:T(1,128)S(1)} %bitcast.4, s32[16,256]{1,0:T(8,128)S(1)} %copy-done.3, ...), custom_call_target="tpu_custom_call" | custom-call | tf_op jit(solution)/shard_map/pallas_call | solution.py:484
  84.7 110.9 %shard_map.101 = bf16[128,4096]{1,0:T(8,128)(2,1)S(1)} custom-call(bf16[16,16,4096]{2,1,0:T(8,128)(2,1)S(1)} %bitcast.3, f32[128,4096]{1,0:T(8,128)S(1)} %get-tuple-element.9.state_ref, f32[16,16,128]{2,1,0:T(8,128)S(1)} %get-tuple-element.10.combine_ref, bf16[1,704,4096]{2,1,0:T(8,128)(2,1)} %gate_hbm.1, bf16[1,704,4096]{2,1,0:T(8,128)(2,1)} %up_hbm.1, ...), custom_call_target="tpu_custom_call" | custom-call | tf_op jit(solution)/shard_map/pallas_call | solution.py:776
  195.7 1.0 copy.12
Async XLA Ops:
  0.0 1.2 copy-start
  1.2 1.2 copy-start.1
  2.5 0.7 copy-start.2
  3.2 0.7 copy-start.3
  3.9 0.7 copy-start.4
  4.6 0.7 copy-start.5

commit v3 on v2

--- a/solution.py
+++ b/solution.py
@@ -11,6 +11,8 @@
 LANES = 4
 PIECES = 4
 GROUPS = 4
+FIRST = 17
+LIMIT = 58
 AHEAD = 2
 SEND_ORDER = (1, 2, 3, 0)
 HOME_ORDER = (2, 3, 1, 0)
@@ -242,18 +244,20 @@
     return value
 
 
-def exchange_kernel(
+def exchange_phase(
     replicas,
+    greet,
     x_hbm,
     w_hbm,
+    small,
+    state_ref,
+    picked_ref,
+    combine_ref,
     residual_ref,
     norm_ref,
     chosen_ref,
     gates_ref,
     place_ref,
-    state_ref,
-    picked_ref,
-    combine_ref,
     lhs,
     rhs,
     side_out,
@@ -365,14 +369,12 @@
         )
         for n, other_side, other_far in blocks
     ]
-    barrier = pltpu.get_barrier_semaphore()
-    partners = [(dp, near), (dp, side), (dp, far)] + [(flip(dp, bit), rank) for bit in bits]
-    for partner in partners:
-        pl.semaphore_signal(barrier, inc=1, device_id=partner, device_id_type=MESH)
     w_load.start()
     for load in x_loads:
         load.start()
-    pl.semaphore_wait(barrier, len(partners))
+    for load in small:
+        load.start()
+    greet()
     for block in blocks[:2]:
         rows_copy(*block).start()
     cols_copy(0).start()
@@ -380,6 +382,8 @@
         rows_copy(*block).start()
     for piece in range(1, PIECES):
         cols_copy(piece).start()
+    for load in small:
+        load.wait()
     routing(
         place_ref[...],
         chosen_ref[...],
@@ -449,70 +453,31 @@
 
     squares = lax.fori_loop(0, PIECES, finish, jnp.zeros((rows, 1), jnp.float32))
     scale = lax.rsqrt(squares / total + 1.0)
-    selector = pick[...].reshape(picked_ref.shape[0], rows).astype(jnp.bfloat16)
+    slots = picked_ref.shape[0] * picked_ref.shape[1]
+    selector = pick[...].reshape(slots, rows).astype(jnp.bfloat16)
     for lane in range(LANES):
         here = slice(lane * (total // LANES), (lane + 1) * (total // LANES))
         normed = (state_ref[:, here] * scale * norm_ref[:, here]).astype(jnp.bfloat16)
-        picked_ref[:, here] = jnp.dot(
-            selector, normed, preferred_element_type=jnp.float32
-        ).astype(picked_ref.dtype)
-    for block in blocks:
-        rows_copy(*block).wait_send()
-
-    def drain(piece, carry):
-        cols_copy(piece).wait_send()
-        for origin in range(replicas):
-            for bit in onward(origin):
-                relay(piece, origin, bit).wait_send()
-            side_copy(piece, origin).wait_send()
-            far_copy(piece, origin).wait_send()
-        return carry
-
-    lax.fori_loop(0, PIECES, drain, 0)
-
-
-def exchange(x, w, residual, norm_gain, chosen, gates, place, replicas, count):
-    rows, columns = residual.shape
-    depth = x.shape[1]
-    width = columns // replicas // PIECES
-    number = replicas * PIECES
-    experts, capacity = chosen.shape
-    most = 2 * capacity // (replicas * count)
-    whole = pl.BlockSpec(memory_space=pltpu.VMEM)
-    outside = pl.BlockSpec(memory_space=pl.ANY)
-    dma = pltpu.SemaphoreType.DMA
-    return pl.pallas_call(
-        functools.partial(exchange_kernel, replicas),
-        out_shape=(
-            jax.ShapeDtypeStruct((rows, columns), jnp.float32),
-            jax.ShapeDtypeStruct((experts * most, columns), jnp.bfloat16),
-            jax.ShapeDtypeStruct((experts, most, rows), jnp.float32),
-        ),
-        in_specs=[outside, outside] + [whole] * 5,
-        out_specs=(whole, whole, whole),
-        scratch_shapes=[
-            pltpu.VMEM((4 * rows, 2 * depth), x.dtype),
-            pltpu.VMEM((2 * depth, columns), w.dtype),
-            pltpu.VMEM((number, 2 * rows, width), jnp.bfloat16),
-            pltpu.VMEM((number, 2 * rows, width), jnp.bfloat16),
-            pltpu.VMEM((number, rows, width), jnp.bfloat16),
-            pltpu.VMEM((number, rows, width), jnp.bfloat16),
-            pltpu.VMEM((experts, most, rows), jnp.float32),
-            dma((5,)),
-            dma((4,)),
-            dma((4,)),
-            dma((PIECES,)),
-            dma((PIECES, replicas)),
-            dma((PIECES, replicas, replicas.bit_length() - 1)),
-            dma((number,)),
-            dma((number,)),
-            dma((number,)),
-            dma((number,)),
-        ],
-        compiler_params=pltpu.CompilerParams(
-            collective_id=2, has_side_effects=True, vmem_limit_bytes=44 * 1024 * 1024
-        ),
-    )(x, w, residual, norm_gain[None, :], chosen, gates, place[None, :])
+        chosen_rows = jnp.dot(selector, normed, preferred_element_type=jnp.float32)
+        picked_ref[:, :, here] = chosen_rows.astype(picked_ref.dtype).reshape(
+            picked_ref.shape[0], picked_ref.shape[1], total // LANES
+        )
+    def settle():
+        for block in blocks:
+            rows_copy(*block).wait_send()
+
+        def drain(piece, carry):
+            cols_copy(piece).wait_send()
+            for origin in range(replicas):
+                for bit in onward(origin):
+                    relay(piece, origin, bit).wait_send()
+                side_copy(piece, origin).wait_send()
+                far_copy(piece, origin).wait_send()
+            return carry
+
+        lax.fori_loop(0, PIECES, drain, 0)
+
+    return settle
 
 
 class Place:
@@ -565,10 +530,10 @@
     lax.fori_loop(start, stop, step, 0)
 
 
-def experts_kernel(
-    replicas,
-    count,
+def experts_phase(
+    at,
     group,
+    greet,
     x_ref,
     state_ref,
     combine_ref,
@@ -592,7 +557,6 @@
     home_sem,
     done_sem,
 ):
-    at = Place(replicas, count)
     most, width = x_ref.shape[1:]
     rows = group * 2 * most
     groups = at.pairs // group
@@ -659,8 +623,9 @@
         pltpu.make_async_copy(hbm.at[0], vmem, weight_sem.at[n])
         for n, (hbm, vmem) in enumerate(((gate_hbm, gate_w), (up_hbm, up_w), (down_hbm, down_w)))
     ]
-    for load in loads:
-        load.start()
+    if greet:
+        for load in loads:
+            load.start()
     own = pltpu.make_async_remote_copy(
         src_ref=x_ref.at[at.pair],
         dst_ref=received.at[0, at.odd],
@@ -669,7 +634,11 @@
         device_id=at.partner,
         device_id_type=MESH,
     )
-    at.greet()
+    if greet:
+        at.greet()
+    else:
+        for load in loads:
+            load.start()
 
     def members(g):
         return max(g * group, 1), (g + 1) * group
@@ -765,36 +734,112 @@
     loop(1, at.pairs, drain)
 
 
+def experts_kernel(replicas, count, group, *refs):
+    experts_phase(Place(replicas, count), group, True, *refs)
+
+
+def experts_scratch(pairs, most, width, hidden_units, dtype):
+    weight = pltpu.VMEM((hidden_units, width), dtype)
+    slots = pltpu.VMEM((pairs, most, width), dtype)
+    sides = pltpu.VMEM((pairs, 2, most, width), dtype)
+    return [
+        weight,
+        weight,
+        weight,
+        sides,
+        sides,
+        slots,
+        slots,
+        pltpu.SemaphoreType.DMA((3,)),
+        pltpu.SemaphoreType.DMA((pairs,)),
+        pltpu.SemaphoreType.DMA((pairs,)),
+        pltpu.SemaphoreType.DMA((pairs, 2)),
+        pltpu.SemaphoreType.DMA((pairs,)),
+        pltpu.SemaphoreType.DMA((pairs,)),
+        pltpu.SemaphoreType.DMA((pairs,)),
+        pltpu.SemaphoreType.DMA((pairs,)),
+    ]
+
+
+def layer_kernel(replicas, count, group, *refs):
+    x_hbm, w_hbm, residual, norm, chosen, gates, place, gate_hbm, up_hbm, down_hbm = refs[:10]
+    out_ref, small_sem, state, picked, combine = refs[10:15]
+    smalls, first, second = refs[15:20], refs[20:20 + FIRST], refs[20 + FIRST:]
+    at = Place(replicas, count)
+    small = [
+        pltpu.make_async_copy(hbm, vmem, small_sem.at[n])
+        for n, (hbm, vmem) in enumerate(zip((residual, norm, chosen, gates, place), smalls))
+    ]
+    settle = exchange_phase(
+        replicas, at.greet, x_hbm, w_hbm, small, state, picked, combine, *smalls, *first
+    )
+    experts_phase(
+        at, group, False, picked, state, combine, gate_hbm, up_hbm, down_hbm, out_ref, *second
+    )
+    settle()
+
+
+def layer(x, w, residual, norm_gain, chosen, gates, place, w_gate, w_up, w_down, replicas, count):
+    rows, columns = residual.shape
+    depth = x.shape[1]
+    width = columns // replicas // PIECES
+    number = replicas * PIECES
+    experts, capacity = chosen.shape
+    most = 2 * capacity // (replicas * count)
+    hidden_units = w_gate.shape[1]
+    half = jnp.bfloat16
+    dma = pltpu.SemaphoreType.DMA
+    arrays = (x, w, residual, norm_gain[None, :], chosen, gates, place[None, :])
+    first = [
+        pltpu.VMEM((4 * rows, 2 * depth), half),
+        pltpu.VMEM((2 * depth, columns), half),
+        pltpu.VMEM((number, 2 * rows, width), half),
+        pltpu.VMEM((number, 2 * rows, width), half),
+        pltpu.VMEM((number, rows, width), half),
+        pltpu.VMEM((number, rows, width), half),
+        pltpu.VMEM((experts, most, rows), jnp.float32),
+        dma((5,)),
+        dma((4,)),
+        dma((4,)),
+        dma((PIECES,)),
+        dma((PIECES, replicas)),
+        dma((PIECES, replicas, replicas.bit_length() - 1)),
+        dma((number,)),
+        dma((number,)),
+        dma((number,)),
+        dma((number,)),
+    ]
+    return pl.pallas_call(
+        functools.partial(layer_kernel, replicas, count, experts // GROUPS),
+        out_shape=jax.ShapeDtypeStruct((rows, columns), half),
+        in_specs=[pl.BlockSpec(memory_space=pltpu.HBM)] * 10,
+        out_specs=pl.BlockSpec(memory_space=pltpu.VMEM),
+        scratch_shapes=[
+            dma((5,)),
+            pltpu.VMEM((rows, columns), jnp.float32),
+            pltpu.VMEM((experts, most, columns), half),
+            pltpu.VMEM((experts, most, rows), jnp.float32),
+        ]
+        + [pltpu.VMEM(array.shape, array.dtype) for array in arrays[2:]]
+        + first
+        + experts_scratch(experts, most, columns, hidden_units, half),
+        compiler_params=pltpu.CompilerParams(
+            collective_id=2, has_side_effects=True, vmem_limit_bytes=LIMIT * 1024 * 1024
+        ),
+    )(*arrays, w_gate, w_up, w_down)
+
+
 def experts_layer(x, state, combine, w_gate, w_up, w_down, replicas, count):
     pairs, most, width = x.shape
     group = pairs // GROUPS
     hidden_units = w_gate.shape[1]
-    weight = pltpu.VMEM((hidden_units, width), w_gate.dtype)
-    slots = pltpu.VMEM((pairs, most, width), x.dtype)
-    sides = pltpu.VMEM((pairs, 2, most, width), x.dtype)
     whole = pl.BlockSpec(memory_space=pltpu.VMEM)
     return pl.pallas_call(
         functools.partial(experts_kernel, replicas, count, group),
         out_shape=jax.ShapeDtypeStruct(state.shape, x.dtype),
         in_specs=[whole] * 3 + [pl.BlockSpec(memory_space=pl.ANY)] * 3,
         out_specs=whole,
-        scratch_shapes=[
-            weight,
-            weight,
-            weight,
-            sides,
-            sides,
-            slots,
-            slots,
-            pltpu.SemaphoreType.DMA((3,)),
-            pltpu.SemaphoreType.DMA((pairs,)),
-            pltpu.SemaphoreType.DMA((pairs,)),
-            pltpu.SemaphoreType.DMA((pairs, 2)),
-            pltpu.SemaphoreType.DMA((pairs,)),
-            pltpu.SemaphoreType.DMA((pairs,)),
-            pltpu.SemaphoreType.DMA((pairs,)),
-            pltpu.SemaphoreType.DMA((pairs,)),
-        ],
+        scratch_shapes=experts_scratch(pairs, most, width, hidden_units, x.dtype),
         compiler_params=pltpu.CompilerParams(
             collective_id=1, has_side_effects=True, vmem_limit_bytes=44 * 1024 * 1024
         ),
@@ -806,10 +851,10 @@
 ):
     count = lax.axis_size("tensor")
     replicas = lax.axis_size("dp")
-    first = exchange if count == 8 and replicas >= 4 else project
-    state, picked, combine = first(
-        head_outputs, out_weight, residual, norm_gain, chosen, gates, place, replicas, count
-    )
+    routed = (head_outputs, out_weight, residual, norm_gain, chosen, gates, place)
+    if count == 8 and replicas >= 4:
+        return layer(*routed, w_gate, w_up, w_down, replicas, count)
+    state, picked, combine = project(*routed, replicas, count)
     experts, most = combine.shape[:2]
     picked = picked.reshape(experts, most, residual.shape[1])
     return experts_layer(picked, state, combine, w_gate, w_up, w_down, replicas, count)

time: 198 us -> 192 us (0.970)
  local copies, waits for them, and re-layouts: 6.23 us -> 2.29 us
    unnamed x13 -> x1, local copies, waits for them, and re-layouts: 6.23 us -> 2.29 us
    pallas_call x2 -> x1, Pallas kernels: 190 us -> 189 us  [layer(): pl.pallas_call(functools.partial(layer_kernel, replicas, count, experts /...]
where the time goes in v3:
time: 192 us; the launch traced here: 191 us
  Pallas kernels  189 us (98%)
  local copies, waits for them, and re-layouts  2.29 us (1%)
    pallas_call x1, Pallas kernels, layer(): pl.pallas_call(functools.partial(layer_kernel, replicas, count, experts /...  189 us

profile of v3, /device:TPU:1, one launch (start us, length us, event | category | flops | bytes accessed | tf_op | source)
XLA Modules:
  0.0 191.1 jit_solution(6252486340433173432)
XLA Ops:
  0.0 188.8 %shard_map.100 = bf16[128,4096]{1,0:T(8,128)(2,1)} custom-call(bf16[1024,512]{1,0:T(8,128)(2,1)} %refs_0_.1, bf16[512,4096]{1,0:T(8,128)(2,1)} %refs_1_.1, bf16[128,4096]{1,0:T(8,128)(2,1)} %refs_2_.1, f32[1,4096]{1,0:T(1,128)} %bitcast.2, s32[16,256]{1,0:T(8,128)} %refs_4_.1, f32[16,256]{1,0:T(8,128)} %refs_5_.1, s32[1,16]{1,0:T(1,128)} %bitcast.3, ...), custom_call_target="tpu_custom_call" | custom-call | tf_op jit(solution)/shard_map/pallas_call | solution.py:812
  188.8 2.3 %copy.12 = bf16[128,4096]{1,0:T(8,128)(2,1)} copy(bf16[128,4096]{1,0:T(8,128)(2,1)} %shard_map.100) | data formatting | bytes 2097152

commit v4 on v3

--- a/solution.py
+++ b/solution.py
@@ -13,10 +13,11 @@
 GROUPS = 4
 FIRST = 17
 LIMIT = 58
+LAG = 2
 AHEAD = 2
 SEND_ORDER = (1, 2, 3, 0)
-HOME_ORDER = (2, 3, 1, 0)
-ISSUE = ((2, (2,)), (3, (3, 1, 0)))
+HOME_ORDER = (2, 1, 3, 0)
+ISSUE = ((2, (2, 1)), (3, (3, 0)))
 
 
 def ring_rank(position, count):
@@ -247,6 +248,7 @@
 def exchange_phase(
     replicas,
     greet,
+    meanwhile,
     x_hbm,
     w_hbm,
     small,
@@ -380,8 +382,8 @@
     cols_copy(0).start()
     for block in blocks[2:]:
         rows_copy(*block).start()
-    for piece in range(1, PIECES):
-        cols_copy(piece).start()
+    cols_copy(1).start()
+    meanwhile()
     for load in small:
         load.wait()
     routing(
@@ -399,10 +401,19 @@
     for block in blocks[:2]:
         rows_copy(*block).wait_recv()
 
-    def begin(piece, origin):
+    def pass_on(piece, origin):
         cols_arrival(piece, origin).wait_recv()
         for bit in onward(origin):
             relay(piece, origin, bit).start()
+        if origin == 0 and isinstance(piece, int) is False or origin == 0 and piece == 1:
+
+            @pl.when(piece + 1 < PIECES)
+            def _():
+                cols_copy(piece + 1).start()
+
+    def begin(piece, origin):
+        if origin > 0:
+            pass_on(piece, origin)
         here = cols(toggled(dp, origin), piece)
         side_out[piece * replicas + origin] = jnp.dot(
             lhs[: 2 * rows, :], rhs[:, here], preferred_element_type=jnp.float32
@@ -419,28 +430,39 @@
         far_copy(piece, origin).start()
         state_ref[:, here] = both[:rows] + residual_ref[:, here].astype(jnp.float32)
 
-    begin(0, 0)
-    begin(0, 1)
+    pass_on(0, 0)
+    for origin in range(LAG):
+        begin(0, origin)
     for block in blocks[2:]:
         rows_copy(*block).wait_recv()
 
     def step(piece, carry):
+        @pl.when(piece == 1)
+        def _():
+            pass_on(1, 0)
+
         for origin in range(replicas):
-            if origin < 2:
+            if origin == 2:
+
+                @pl.when((piece > 0) & (piece + 1 < PIECES))
+                def _():
+                    pass_on(piece + 1, 0)
+
+            if origin < LAG:
 
                 @pl.when(piece > 0)
                 def _():
                     begin(piece, origin)
-                    middle(piece - 1, origin + replicas - 2)
+                    middle(piece - 1, origin + replicas - LAG)
 
             else:
                 begin(piece, origin)
-                middle(piece, origin - 2)
+                middle(piece, origin - LAG)
         return carry
 
     lax.fori_loop(0, PIECES, step, 0)
-    middle(PIECES - 1, replicas - 2)
-    middle(PIECES - 1, replicas - 1)
+    for origin in range(replicas - LAG, replicas):
+        middle(PIECES - 1, origin)
 
     def finish(piece, squares):
         for origin in range(replicas):
@@ -528,6 +550,13 @@
         return carry
 
     lax.fori_loop(start, stop, step, 0)
+
+
+def weight_loads(gate_hbm, up_hbm, down_hbm, gate_w, up_w, down_w, weight_sem):
+    return [
+        pltpu.make_async_copy(hbm.at[0], vmem, weight_sem.at[n])
+        for n, (hbm, vmem) in enumerate(((gate_hbm, gate_w), (up_hbm, up_w), (down_hbm, down_w)))
+    ]
 
 
 def experts_phase(
@@ -619,10 +648,7 @@
         add(k)
         home(k).start()
 
-    loads = [
-        pltpu.make_async_copy(hbm.at[0], vmem, weight_sem.at[n])
-        for n, (hbm, vmem) in enumerate(((gate_hbm, gate_w), (up_hbm, up_w), (down_hbm, down_w)))
-    ]
+    loads = weight_loads(gate_hbm, up_hbm, down_hbm, gate_w, up_w, down_w, weight_sem)
     if greet:
         for load in loads:
             load.start()
@@ -636,9 +662,6 @@
     )
     if greet:
         at.greet()
-    else:
-        for load in loads:
-            load.start()
 
     def members(g):
         return max(g * group, 1), (g + 1) * group
@@ -655,13 +678,18 @@
 
     def step(g, carry):
         first = g * group
-        start = first + AHEAD * group
 
         def forward_piece(piece):
-            @pl.when(g + AHEAD < GROUPS)
+            @pl.when(g == 0)
             def _():
-                cut = [start + n * group // PIECES for n in (piece, piece + 1)]
-                loop(cut[0], cut[1], forward)
+                cut = [n * group // PIECES for n in (piece, piece + 1)]
+                loop(AHEAD * group + cut[0], AHEAD * group + cut[1], forward)
+
+            @pl.when((g > 0) & (g < GROUPS - 1))
+            def _():
+                turn = (g - 1) * PIECES + piece
+                cut = [n * group // (2 * PIECES) for n in (turn, turn + 1)]
+                loop((AHEAD + 1) * group + cut[0], (AHEAD + 1) * group + cut[1], forward)
 
         loop(first, first + group, lambda k: sideways(k, 1 - at.odd).wait_recv())
         x = received[pl.ds(first, group)].reshape(rows, width)
@@ -770,8 +798,13 @@
         pltpu.make_async_copy(hbm, vmem, small_sem.at[n])
         for n, (hbm, vmem) in enumerate(zip((residual, norm, chosen, gates, place), smalls))
     ]
+
+    def meanwhile():
+        for load in weight_loads(gate_hbm, up_hbm, down_hbm, *second[:3], second[7]):
+            load.start()
+
     settle = exchange_phase(
-        replicas, at.greet, x_hbm, w_hbm, small, state, picked, combine, *smalls, *first
+        replicas, at.greet, meanwhile, x_hbm, w_hbm, small, state, picked, combine, *smalls, *first
     )
     experts_phase(
         at, group, False, picked, state, combine, gate_hbm, up_hbm, down_hbm, out_ref, *second

time: 192 us -> 191 us (level)
  Pallas kernels: 189 us -> 187 us
where the time goes in v4:
time: 191 us; the launch traced here: 190 us
  Pallas kernels  187 us (98%)
  local copies, waits for them, and re-layouts  2.29 us (1%)
    pallas_call x1, Pallas kernels, layer(): pl.pallas_call(functools.partial(layer_kernel, replicas, count, experts /...  187 us

profile of v4, /device:TPU:1, one launch (start us, length us, event | category | flops | bytes accessed | tf_op | source)
XLA Modules:
  0.0 189.7 jit_solution(905628380746378741)
XLA Ops:
  0.0 187.4 %shard_map.100 = bf16[128,4096]{1,0:T(8,128)(2,1)} custom-call(bf16[1024,512]{1,0:T(8,128)(2,1)} %refs_0_.1, bf16[512,4096]{1,0:T(8,128)(2,1)} %refs_1_.1, bf16[128,4096]{1,0:T(8,128)(2,1)} %refs_2_.1, f32[1,4096]{1,0:T(1,128)} %bitcast.2, s32[16,256]{1,0:T(8,128)} %refs_4_.1, f32[16,256]{1,0:T(8,128)} %refs_5_.1, s32[1,16]{1,0:T(1,128)} %bitcast.3, ...), custom_call_target="tpu_custom_call" | custom-call | tf_op jit(solution)/shard_map/pallas_call | solution.py:845
  187.4 2.3 %copy.12 = bf16[128,4096]{1,0:T(8,128)(2,1)} copy(bf16[128,4096]{1,0:T(8,128)(2,1)} %shard_map.100) | data formatting | bytes 2097152
